TPU v7x, 256 devices: a whole 4x4x8 slice. The times are simulated.
256 devices in a mesh: grp: 64 (over y, x, z_lo, core), blk: 4 (over z_hi).
Axes of the slice: x: 4, y: 4, z: 8 (z_hi: 4, z_lo: 2; z = z_hi * 2 + z_lo), core: 2. Of those that a mesh axis runs over, the one named last changes fastest.
Arguments:
- tokens: bfloat16 [2048, 6144], P(('grp', 'blk')), may hold values from -6 to 6
- norm_gain: bfloat16 [6144], replicated, may hold values from 0.099609375 to 1.8984375
- expert_ids: int32 [2048, 2], P(('grp', 'blk')), may hold values from 0 to 7, all different within a row; in each aligned block of 8 rows (0 to 7, 8 to 15, ...) at most 3 rows name the same one
- combine: float32 [2048, 2], P(('grp', 'blk')), may hold values from 0.2 to 1
- w_gate: bfloat16 [6144, 65536], P(None, ('grp', 'blk')), may hold values from -0.078125 to 0.078125
- w_up: bfloat16 [6144, 65536], P(None, ('grp', 'blk')), may hold values from -0.078125 to 0.078125
- w_down: bfloat16 [65536, 6144], P(('grp', 'blk')), may hold values from -0.0625 to 0.0625
Outputs:
- layer_out: bfloat16 [2048, 6144], P(('grp', 'blk'))
Inputs may be any that keep to these rules, and one draw needn't show every extreme that they name: `expert_ids`: each row names 2 different experts; in the rows of one device no expert is named more than 3 times, a bound that some block reaches.
All inputs are finite; a program needn't handle non-finite values.
Results may differ from a plain program's by a relative error of at most 0.0075.
Values may be sent and summed in bfloat16 or wider, within the bound.
A program may use at most 128 MiB of HBM per device.

v0:
```python
import jax
import jax.numpy as jnp
from jax import lax
from jax.sharding import PartitionSpec as P

E = 8
TOP = 2
CAP = 3
epsilon = 1e-05


def in_order(blocks, dim):
    dims = list(blocks.shape[1:])
    dims[dim] *= blocks.shape[0]
    return jnp.moveaxis(blocks, 0, dim).reshape(dims)


def copy_for_each(x, axis):
    count = lax.axis_size(axis)
    return lax.all_to_all(jnp.broadcast_to(x[None], (count, *x.shape)), axis, 0, 0, tiled=True)


def gathered_copies(x, axis, dim):
    return in_order(copy_for_each(x, axis), dim)


def on_device(tokens, norm_gain, expert_ids, combine, w_gate, w_up, w_down):
    group_count = lax.axis_size("grp")
    per_group = group_count // E
    tok_count = tokens.shape[0]
    model_width = tokens.shape[1]
    wide_tokens = tokens.astype(jnp.float32)
    scale_rows = lax.rsqrt(jnp.mean(wide_tokens * wide_tokens, axis=1, keepdims=True) + epsilon)
    normed = (wide_tokens * scale_rows * norm_gain.astype(jnp.float32)[None, :]).astype(
        jnp.bfloat16
    )
    pair_rows = jnp.repeat(normed, TOP, axis=0)
    route_ids = expert_ids.reshape(tok_count * TOP)
    one_hot = (route_ids[:, None] == jnp.arange(E, dtype=jnp.int32)[None, :]).astype(jnp.int32)
    earlier = jnp.cumsum(one_hot, axis=0) - one_hot
    slot_index = jnp.sum(earlier * one_hot, axis=1)
    slot_match = (
        slot_index[None, None, :] == jnp.arange(CAP, dtype=jnp.int32)[None, :, None]
    ).astype(jnp.int32)
    placer = (one_hot.T[:, None, :] * slot_match).astype(jnp.bfloat16)
    buffer = jnp.einsum(
        "ecp,pd->ecd", placer, pair_rows, preferred_element_type=jnp.float32
    ).astype(jnp.bfloat16)
    stacked = gathered_copies(buffer[None], "blk", 0)
    outgoing = jnp.repeat(stacked, per_group, axis=1)
    arrived = lax.all_to_all(outgoing, "grp", split_axis=1, concat_axis=1, tiled=True)
    shard_rows = arrived.reshape(-1, model_width)
    gate_val = jnp.dot(shard_rows, w_gate, preferred_element_type=jnp.float32)
    up_val = jnp.dot(shard_rows, w_up, preferred_element_type=jnp.float32)
    hidden = (jax.nn.silu(gate_val) * up_val).astype(jnp.bfloat16)
    partial_value = jnp.dot(hidden, w_down, preferred_element_type=jnp.float32)
    rounded = lax.optimization_barrier(partial_value.astype(jnp.bfloat16))
    own_rows = lax.psum_scatter(
        rounded.astype(jnp.float32).astype(jnp.bfloat16), "blk", scatter_dimension=0, tiled=True
    ).astype(jnp.float32)
    home_terms = own_rows.reshape(group_count, CAP, model_width)
    returned = lax.all_to_all(
        home_terms.astype(jnp.bfloat16), "grp", split_axis=0, concat_axis=0, tiled=True
    ).astype(home_terms.dtype)
    expert_out = jnp.sum(returned.reshape(E, per_group, CAP, model_width), axis=1)
    pair_out = expert_out.reshape(E * CAP, model_width)[route_ids * CAP + slot_index]
    expert_mix = jnp.sum(
        pair_out.reshape(tok_count, TOP, model_width) * combine[:, :, None], axis=1
    )
    return (wide_tokens + expert_mix).astype(jnp.bfloat16)


def solution(mesh):
    return jax.shard_map(
        on_device,
        mesh=mesh,
        in_specs=(
            P(("grp", "blk"), None),
            P(),
            P(("grp", "blk"), None),
            P(("grp", "blk"), None),
            P(None, ("grp", "blk")),
            P(None, ("grp", "blk")),
            P(("grp", "blk"), None),
        ),
        out_specs=P(("grp", "blk"), None),
        check_vma=False,
    )
```

profile of v0, /device:TPU:1, one launch (start us, length us, event | category | flops | bytes accessed | tf_op | source)
XLA Modules:
  0.0 489.2 jit_solution(17626698553006937303)
XLA Ops:
  6.5 0.9 copy.16
  7.4 0.1 eq.44
  7.5 0.1 fusion.5
  7.6 0.2 select_reduce_fusion
  7.8 0.7 convert_element_type.55
  8.5 1.1 fusion.1
  9.6 1.0 fusion.3
  10.6 0.1 broadcast_in_dim.6
  10.7 0.1 reshape.134
  10.8 0.2 convolution_convert_fusion.1
  11.0 0.1 broadcast_in_dim.7
  11.1 36.6 %all_to_all.15 = bf16[4,1,8,3,6144]{4,2,3,1,0:T(8,128)(2,1)S(1)} all-to-all(bf16[4,1,8,3,6144]{4,2,3,1,0:T(8,128)(2,1)S(1)} %broadcast_in_dim.7), channel_id=1, replica_groups=mesh['grp'=64,'blk'=4] {'blk'}, dimensions={0} | all-to-all | bytes 2359296 | tf_op jit(solution)/shard_map/all_to_all | solution.py:20
  47.7 0.9 copy.17
  48.6 4.6 broadcast_in_dim.8
  53.3 119.6 %all_to_all.16 = bf16[4,64,3,6144]{3,0,2,1:T(4,128)(2,1)S(1)} all-to-all(bf16[4,64,3,6144]{3,0,2,1:T(4,128)(2,1)S(1)} %bitcast.26), channel_id=1, replica_groups=mesh['grp'=64,'blk'=4] {'grp'}, dimensions={1} | all-to-all | bytes 18874368 | tf_op jit(solution)/shard_map/all_to_all | solution.py:51
  172.8 25.3 %copy.18 = bf16[4,64,3,6144]{3,2,1,0:T(4,128)(2,1)} copy(bf16[4,64,3,6144]{3,0,2,1:T(4,128)(2,1)S(1)} %all_to_all.16) | data formatting | bytes 18874368 | tf_op jit(solution)/shard_map/all_to_all | solution.py:51
  198.2 23.5 %reshape.119 = bf16[768,6144]{1,0:T(8,128)(2,1)} reshape(bf16[4,64,3,6144]{3,2,1,0:T(4,128)(2,1)} %copy.18) | data formatting | bytes 18874368 | tf_op jit(solution)/shard_map/reshape | solution.py:52
  221.7 8.1 %fusion.11 = f32[768,256]{1,0:T(8,128)} fusion(bf16[768,6144]{1,0:T(8,128)(2,1)} %reshape.119, bf16[6144,256]{1,0:T(8,128)(2,1)} %param.11), kind=kOutput, calls=%fused_computation.30 | convolution fusion | flops 2415919104 | bytes 13369344 | tf_op jit(solution)/shard_map/dot_general | solution.py:53
  229.7 19.4 %convolution_convert_fusion = bf16[768,6144]{1,0:T(8,128)(2,1)} fusion(bf16[256,6144]{1,0:T(8,128)(2,1)S(1)} %copy-done, bf16[768,6144]{1,0:T(8,128)(2,1)} %reshape.119, bf16[6144,256]{1,0:T(8,128)(2,1)} %param.12, f32[768,256]{1,0:T(8,128)} %fusion.11), kind=kOutput, calls=%fused_computation.1 | convolution fusion | flops 4837736448 | bytes 25952256 | tf_op jit(solution)/shard_map/dot_general | solution.py:56
  249.1 163.2 %reduce-scatter.2.cloned.1.call-done = bf16[192,6144]{1,0:T(8,128)(2,1)} async-done(((bf16[768,6144]{1,0:T(8,128)(2,1)}), bf16[192,6144]{1,0:T(8,128)(2,1)}) %reduce-scatter.2.cloned.1.call-update) | async-done | bytes 2359312 | tf_op jit(solution)/shard_map/reduce_scatter | solution.py:58
  412.3 6.5 %convert_element_type.60 = bf16[64,3,6144]{2,1,0:T(4,128)(2,1)} reshape(bf16[192,6144]{1,0:T(8,128)(2,1)} %reduce-scatter.2.cloned.1.call-done) | data formatting | bytes 4718592 | tf_op jit(solution)/shard_map/convert_element_type | solution.py:63
  418.8 9.2 %all-to-all-start.2 = ((bf16[64,3,6144]{2,1,0:T(4,128)(2,1)}), bf16[64,3,6144]{2,1,0:T(4,128)(2,1)}, u32[]{:S(2)}, u32[]{:S(2)}) async-start(bf16[64,3,6144]{2,1,0:T(4,128)(2,1)} %convert_element_type.60), calls=%async_computation.3 | async-start | bytes 6291456 | tf_op jit(solution)/shard_map/all_to_all | solution.py:62
  428.0 0.1 copy.19
  428.1 0.1 mul.75
  428.2 0.1 copy.20
  428.3 41.3 %all-to-all-done.2 = bf16[64,3,6144]{2,1,0:T(4,128)(2,1)} async-done(((bf16[64,3,6144]{2,1,0:T(4,128)(2,1)}), bf16[64,3,6144]{2,1,0:T(4,128)(2,1)}, u32[]{:S(2)}, u32[]{:S(2)}) %all-to-all-start.2) | async-done | bytes 2359328 | tf_op jit(solution)/shard_map/all_to_all | solution.py:62
  469.6 4.5 convert_reduce_fusion
  474.1 2.2 reshape.122
  476.4 2.6 gather_fusion
  479.0 1.2 reshape.123
  480.2 0.6 multiply_reduce_fusion
  480.8 1.6 fusion.4
  (15 shorter events, 0.1 us)
Async XLA Ops:
  6.5 223.2 %copy-start = (bf16[256,6144]{1,0:T(8,128)(2,1)S(1)}, bf16[256,6144]{1,0:T(8,128)(2,1)}, u32[]{:S(2)}) copy-start(bf16[256,6144]{1,0:T(8,128)(2,1)} %param.13) | copy-start | bytes 9437188
  6.5 405.8 %reduce-scatter.2.cloned.1.call-start = ((), (), s32[]{:S(2)}) async-start(), calls=%async_computation.4 | async-start | bytes 11796480 | tf_op jit(solution)/shard_map/reduce_scatter | solution.py:58
  418.8 9.2 %copy-start.1 = (s32[8,2]{0,1:T(2,128)S(1)}, s32[8,2]{0,1:T(2,128)}, u32[]{:S(2)}) copy-start(s32[8,2]{0,1:T(2,128)} %param.9) | copy-start | bytes 196
  418.8 9.4 %copy-start.2 = (f32[8,2]{0,1:T(2,128)S(1)}, f32[8,2]{0,1:T(2,128)}, u32[]{:S(2)}) copy-start(f32[8,2]{0,1:T(2,128)} %param.10) | copy-start | bytes 196
  418.8 50.8 %all-to-all-start.2 = ((bf16[64,3,6144]{2,1,0:T(4,128)(2,1)}), bf16[64,3,6144]{2,1,0:T(4,128)(2,1)}, u32[]{:S(2)}, u32[]{:S(2)}) async-start(bf16[64,3,6144]{2,1,0:T(4,128)(2,1)} %convert_element_type.60), calls=%async_computation.3 | async-start | bytes 6291456 | tf_op jit(solution)/shard_map/all_to_all | solution.py:62
Sparse Core Ops, SparseCore 0:
  249.3 163.0 reduce-scatter.1
where the time goes:
time: 490 us; the launch traced here: 489 us
  waiting for transfers between devices  205 us (42%)
  blocking collectives  156 us (32%)
  local copies, waits for them, and re-layouts  68.5 us (14%)
  matrix products  27.6 us (6%)
  between operations  13.5 us (3%)
  other arithmetic  9.71 us (2%)
  starting transfers between devices  9.16 us (2%)
    reduce_scatter x1, waiting for transfers between devices, on_device(): lax.psum_scatter(rounded.astype(jnp.float32).astype(jnp.bfloat16), 'blk',...  163 us
    all_to_all x1, blocking collectives, on_device(): lax.all_to_all(outgoing, 'grp', split_axis=1, concat_axis=1, tiled=True)  120 us
    all_to_all x1, waiting for transfers between devices, on_device(): lax.all_to_all(home_terms.astype(jnp.bfloat16), 'grp', split_axis=0, conc...  41.3 us
    all_to_all x1, blocking collectives, copy_for_each(): lax.all_to_all(jnp.broadcast_to(x[None], (count, *x.shape)), axis, 0, 0,...  36.6 us
    all_to_all x1, local copies, waits for them, and re-layouts, on_device(): lax.all_to_all(outgoing, 'grp', split_axis=1, concat_axis=1, tiled=True)  25.3 us
    reshape x1, local copies, waits for them, and re-layouts, on_device(): shard_rows = arrived.reshape(-1, model_width)  23.5 us
    dot_general x1, matrix products, on_device(): partial_value = jnp.dot(hidden, w_down, preferred_element_type=jnp.float32)  19.4 us
  transfers between devices with their start and end apart: 2, of which 2 were waited for; matrix products, arithmetic and copies ran while one was open for 0% of the time, Pallas kernels for 0%

commit v1 on v0

--- a/solution.py
+++ b/solution.py
@@ -48,7 +48,10 @@
     ).astype(jnp.bfloat16)
     stacked = gathered_copies(buffer[None], "blk", 0)
     outgoing = jnp.repeat(stacked, per_group, axis=1)
-    arrived = lax.all_to_all(outgoing, "grp", split_axis=1, concat_axis=1, tiled=True)
+    arrived = jnp.concatenate(
+        lax.all_to_all(jnp.stack(jnp.split(outgoing, lax.axis_size("grp"), axis=1)), "grp", 0, 0),
+        axis=1,
+    )
     shard_rows = arrived.reshape(-1, model_width)
     gate_val = jnp.dot(shard_rows, w_gate, preferred_element_type=jnp.float32)
     up_val = jnp.dot(shard_rows, w_up, preferred_element_type=jnp.float32)

time: 490 us -> 496 us (1.012)
    all_to_all x1 -> x0, local copies, waits for them, and re-layouts: 25.3 us -> none  [on_device(): lax.all_to_all(outgoing, 'grp', split_axis=1, concat_axis=1, tiled=True)]
    another operation x0 -> x2, local copies, waits for them, and re-layouts: none -> 23.6 us  [the longest x1 23.5 us: on_device(): shard_rows = arrived.reshape(-1, model_width)]
where the time goes in v1:
time: 496 us; the launch traced here: 494 us
  waiting for transfers between devices  205 us (41%)
  blocking collectives  156 us (31%)
  local copies, waits for them, and re-layouts  73 us (15%)
  matrix products  27.6 us (6%)
  between operations  13.6 us (3%)
  other arithmetic  9.71 us (2%)
  starting transfers between devices  9.23 us (2%)
    reduce_scatter x1, waiting for transfers between devices, on_device(): lax.psum_scatter(rounded.astype(jnp.float32).astype(jnp.bfloat16), 'blk',...  164 us
    all_to_all x1, blocking collectives, on_device(): lax.all_to_all(jnp.stack(jnp.split(outgoing, lax.axis_size('grp'), axis=1...  120 us
    all_to_all x1, waiting for transfers between devices, on_device(): lax.all_to_all(home_terms.astype(jnp.bfloat16), 'grp', split_axis=0, conc...  41.3 us
    all_to_all x1, blocking collectives, copy_for_each(): lax.all_to_all(jnp.broadcast_to(x[None], (count, *x.shape)), axis, 0, 0,...  36.6 us
    reshape x1, local copies, waits for them, and re-layouts, on_device(): jnp.concatenate(lax.all_to_all(jnp.stack(jnp.split(outgoing, lax.axis_siz...  25.3 us
    another operation x1, local copies, waits for them, and re-layouts, on_device(): shard_rows = arrived.reshape(-1, model_width)  23.5 us
    dot_general x1, matrix products, on_device(): partial_value = jnp.dot(hidden, w_down, preferred_element_type=jnp.float32)  19.4 us
  transfers between devices with their start and end apart: 2, of which 2 were waited for; matrix products, arithmetic and copies ran while one was open for 0% of the time, Pallas kernels for 0%

profile of v1, /device:TPU:1, one launch (start us, length us, event | category | flops | bytes accessed | tf_op | source)
XLA Modules:
  0.0 494.5 jit_solution(17764920771073616513)
XLA Ops:
  6.5 0.9 copy.142
  7.4 0.1 eq.44
  7.5 0.1 fusion.69
  7.6 0.2 select_reduce_fusion
  7.8 0.7 convert_element_type.55
  8.5 1.1 fusion.1
  9.6 1.0 fusion.3
  10.6 0.1 broadcast_in_dim.6
  10.7 0.1 reshape.134
  10.8 0.2 convolution_convert_fusion.1
  11.0 0.1 broadcast_in_dim.7
  11.1 36.6 %all_to_all.15 = bf16[4,1,8,3,6144]{4,2,3,1,0:T(8,128)(2,1)S(1)} all-to-all(bf16[4,1,8,3,6144]{4,2,3,1,0:T(8,128)(2,1)S(1)} %broadcast_in_dim.7), channel_id=1, replica_groups=mesh['grp'=64,'blk'=4] {'blk'}, dimensions={0} | all-to-all | bytes 2359296 | tf_op jit(solution)/shard_map/all_to_all | solution.py:20
  47.7 0.9 copy.143
  48.6 4.6 broadcast_in_dim.8
  57.8 119.6 %all_to_all.16 = bf16[64,4,1,3,6144]{4,1,3,2,0:T(4,128)(2,1)S(1)} all-to-all(bf16[64,4,1,3,6144]{4,1,3,2,0:T(4,128)(2,1)S(1)} %fusion.5), channel_id=1, replica_groups=mesh['grp'=64,'blk'=4] {'grp'}, dimensions={0} | all-to-all | bytes 18874368 | tf_op jit(solution)/shard_map/all_to_all | solution.py:52
  177.4 25.3 %copy.144 = bf16[4,64,1,3,6144]{4,3,1,0,2:T(4,128)(2,1)} copy(bf16[4,64,1,3,6144]{4,0,3,2,1:T(4,128)(2,1)S(1)} %bitcast.285) | data formatting | bytes 18874368 | tf_op jit(solution)/shard_map/reshape | solution.py:51
  202.7 23.5 %reshape_reshape.3 = bf16[768,6144]{1,0:T(8,128)(2,1)} reshape(bf16[4,64,1,3,6144]{4,3,1,0,2:T(4,128)(2,1)} %copy.144) | data formatting | bytes 18874368 | tf_op jit(solution)/shard_map/reshape;reshape | solution.py:55
  226.2 8.1 %fusion.75 = f32[768,256]{1,0:T(8,128)} fusion(bf16[768,6144]{1,0:T(8,128)(2,1)} %reshape_reshape.3, bf16[6144,256]{1,0:T(8,128)(2,1)} %param.11), kind=kOutput, calls=%fused_computation.158 | convolution fusion | flops 2415919104 | bytes 13369344 | tf_op jit(solution)/shard_map/dot_general | solution.py:56
  234.3 19.4 %convolution_convert_fusion = bf16[768,6144]{1,0:T(8,128)(2,1)} fusion(bf16[256,6144]{1,0:T(8,128)(2,1)S(1)} %copy-done, bf16[768,6144]{1,0:T(8,128)(2,1)} %reshape_reshape.3, bf16[6144,256]{1,0:T(8,128)(2,1)} %param.12, f32[768,256]{1,0:T(8,128)} %fusion.75), kind=kOutput, calls=%fused_computation.1 | convolution fusion | flops 4837736448 | bytes 25952256 | tf_op jit(solution)/shard_map/dot_general | solution.py:59
  253.7 163.8 %reduce-scatter.2.cloned.1.call-done = bf16[192,6144]{1,0:T(8,128)(2,1)} async-done(((bf16[768,6144]{1,0:T(8,128)(2,1)}), bf16[192,6144]{1,0:T(8,128)(2,1)}) %reduce-scatter.2.cloned.1.call-update) | async-done | bytes 2359312 | tf_op jit(solution)/shard_map/reduce_scatter | solution.py:61
  417.6 6.5 %convert_element_type.60 = bf16[64,3,6144]{2,1,0:T(4,128)(2,1)} reshape(bf16[192,6144]{1,0:T(8,128)(2,1)} %reduce-scatter.2.cloned.1.call-done) | data formatting | bytes 4718592 | tf_op jit(solution)/shard_map/convert_element_type | solution.py:66
  424.0 9.2 %all-to-all-start.2 = ((bf16[64,3,6144]{2,1,0:T(4,128)(2,1)}), bf16[64,3,6144]{2,1,0:T(4,128)(2,1)}, u32[]{:S(2)}, u32[]{:S(2)}) async-start(bf16[64,3,6144]{2,1,0:T(4,128)(2,1)} %convert_element_type.60), calls=%async_computation.3 | async-start | bytes 6291456 | tf_op jit(solution)/shard_map/all_to_all | solution.py:65
  433.3 0.1 copy.145
  433.4 0.1 mul.75
  433.5 0.1 copy.146
  433.6 41.3 %all-to-all-done.2 = bf16[64,3,6144]{2,1,0:T(4,128)(2,1)} async-done(((bf16[64,3,6144]{2,1,0:T(4,128)(2,1)}), bf16[64,3,6144]{2,1,0:T(4,128)(2,1)}, u32[]{:S(2)}, u32[]{:S(2)}) %all-to-all-start.2) | async-done | bytes 2359328 | tf_op jit(solution)/shard_map/all_to_all | solution.py:65
  474.9 4.5 convert_reduce_fusion
  479.4 2.2 reshape.122
  481.6 2.6 gather_fusion
  484.3 1.2 reshape.123
  485.5 0.6 multiply_reduce_fusion
  486.1 1.6 fusion.4
  (79 shorter events, 4.6 us)
Async XLA Ops:
  6.5 227.8 %copy-start = (bf16[256,6144]{1,0:T(8,128)(2,1)S(1)}, bf16[256,6144]{1,0:T(8,128)(2,1)}, u32[]{:S(2)}) copy-start(bf16[256,6144]{1,0:T(8,128)(2,1)} %param.13) | copy-start | bytes 9437188
  6.5 411.0 %reduce-scatter.2.cloned.1.call-start = ((), (), s32[]{:S(2)}) async-start(), calls=%async_computation.4 | async-start | bytes 11796480 | tf_op jit(solution)/shard_map/reduce_scatter | solution.py:61
  253.7 179.6 %copy-start.1 = (s32[8,2]{0,1:T(2,128)S(1)}, s32[8,2]{0,1:T(2,128)}, u32[]{:S(2)}) copy-start(s32[8,2]{0,1:T(2,128)} %param.9) | copy-start | bytes 196
  253.7 179.8 %copy-start.2 = (f32[8,2]{0,1:T(2,128)S(1)}, f32[8,2]{0,1:T(2,128)}, u32[]{:S(2)}) copy-start(f32[8,2]{0,1:T(2,128)} %param.10) | copy-start | bytes 196
  424.0 50.8 %all-to-all-start.2 = ((bf16[64,3,6144]{2,1,0:T(4,128)(2,1)}), bf16[64,3,6144]{2,1,0:T(4,128)(2,1)}, u32[]{:S(2)}, u32[]{:S(2)}) async-start(bf16[64,3,6144]{2,1,0:T(4,128)(2,1)} %convert_element_type.60), calls=%async_computation.3 | async-start | bytes 6291456 | tf_op jit(solution)/shard_map/all_to_all | solution.py:65
Sparse Core Ops, SparseCore 0:
  253.8 163.6 reduce-scatter.1
